TPU v7x, 32 devices: a whole 2x2x4 slice. The times are simulated.
32 devices in a mesh: tm: 8 (over z, y), sym: 4 (over x, core).
Axes of the slice: x: 2, y: 2, z: 4, core: 2. Of those that a mesh axis runs over, the one named last changes fastest.
Arguments:
- trade_age: float32 [65536], P(('tm', 'sym')), may hold values from 0.02 to 20
- trade_size: float32 [65536], P(('tm', 'sym')), may hold values from 0.5 to 4
- owner: int32 [65536, 1], P(('tm', 'sym')), may hold values from 0 to 31; in each aligned block of 2048 rows (0 to 2047, 2048 to 4095, ...) at most 96 rows name the same one
- symbol_lane: int32 [65536], P(('tm', 'sym')), may hold values from 0 to 15
- quote_offset: int32 [65536], P(('tm', 'sym')), may hold values from 0 to 511
- quotes: float32 [64, 4096, 128], P('sym', 'tm'), may hold values from -6 to 6
- rates: float32 [128], replicated, may hold values from 0.05 to 2
Outputs:
- joined: float32 [65536, 128], P(('tm', 'sym'))
Inputs may be any that keep to these rules, and one draw needn't show every extreme that they name: Among the 2048 trades of one device no owner is named more than 96 times, and in every draw some device names some owner exactly 96 times. Owner o holds symbols of group o % 4 and quote rows of block o // 4.
All inputs are finite; a program needn't handle non-finite values.
Results may differ from a plain program's by a relative error of at most 0.00002.
Values sent between devices are 32-bit elements; how exact they have to be, the bound alone decides.
A program may use at most 64 MiB of HBM per device.

v0:
```python
import functools

import jax
import jax.numpy as jnp
from jax import lax
from jax.experimental import pallas as pl
from jax.experimental.pallas import tpu as pltpu
from jax.sharding import PartitionSpec as P

LANES = 128
PAD = 8
MESH = pl.DeviceIdType.MESH


def flips(me, devices):
    out, bit = [], 1
    while bit < devices:
        out.append(bit - 2 * bit * lax.rem(lax.div(me, bit), 2))
        bit *= 2
    return out


def join_kernel(
    cfg,
    owner_ref, lane_ref, offset_ref, age_ref, rates_ref, quotes_ref,
    out_ref,
    table, recv, sbuf, msg, got, rows_v, rows_s, slot_v, slot_s, cur, prev, bsend, brecv,
    qsem, bsem, msend, mrecv, jsend, jrecv, ssem,
):
    tm_n, sym_n, cap = cfg
    devices = tm_n * sym_n
    ticks = owner_ref.shape[1]
    lane_count, quote_rows, features = quotes_ref.shape
    stride = quote_rows + PAD
    tm, sym = lax.axis_index("tm"), lax.axis_index("sym")
    me = tm * sym_n + sym

    flip = flips(me, devices)
    group = min(8, devices)

    top = len(flip) - 1
    half = lax.div(2 * me, devices)
    quarter = lax.rem(lax.div(4 * me, devices), 2)

    def peer(k):
        p = me
        for i, step in enumerate(flip):
            if i == top - 1 and k >> top & 1:
                want = 1 - half if k >> i & 1 else half
                p = p + (want - quarter) * (1 << i)
            elif k >> i & 1:
                p = p + step
        return p

    def device(p):
        return (lax.div(p, sym_n), lax.rem(p, sym_n))

    everyone = range(devices - 1, 0, -1)

    loads = [
        pltpu.make_async_copy(
            quotes_ref.at[lane], table.at[pl.ds(lane * stride + PAD, quote_rows)], qsem.at[lane]
        )
        for lane in range(lane_count)
    ]
    for load in loads:
        load.start()

    barrier = pltpu.get_barrier_semaphore()

    for k in everyone:
        pl.semaphore_signal(barrier, inc=1, device_id=device(peer(k)), device_id_type=MESH)

    owner = owner_ref[...]
    mine = owner == lax.broadcasted_iota(jnp.int32, (devices, ticks), 0)
    hot = mine.astype(jnp.float32)
    hot_b = hot.astype(jnp.bfloat16)
    width = 256 if ticks % 256 == 0 else 128
    upper = (
        lax.broadcasted_iota(jnp.int32, (width, width), 0)
        < lax.broadcasted_iota(jnp.int32, (width, width), 1)
    ).astype(jnp.float32).astype(jnp.bfloat16)
    base = jnp.zeros((devices, 1), jnp.float32)
    ranks = []
    for start in range(0, ticks, width):
        part = hot[:, start:start + width]
        before = jnp.dot(
            hot_b[:, start:start + width], upper, preferred_element_type=jnp.float32
        )
        ranks.append(jnp.sum(part * (before + base), axis=0, keepdims=True))
        base = base + jnp.sum(part, axis=1, keepdims=True)
    rank = jnp.concatenate(ranks, axis=1)
    slot_v[...] = jnp.clip(owner * cap + rank.astype(jnp.int32), 0, devices * cap - 1)
    slot_copy = pltpu.make_async_copy(slot_v, slot_s, ssem.at[0])
    slot_copy.start()

    place = (
        rank.astype(jnp.int32) == lax.broadcasted_iota(jnp.int32, (LANES, ticks), 0)
    ).astype(jnp.float32).astype(jnp.bfloat16)
    local = lane_ref[...] * stride + PAD - 1 + offset_ref[...]
    age = age_ref[...]
    high = age.astype(jnp.bfloat16).astype(jnp.float32)
    middle = (age - high).astype(jnp.bfloat16).astype(jnp.float32)
    low = age - high - middle
    pieces = [
        (local // LANES).astype(jnp.float32), (local % LANES).astype(jnp.float32), high, middle, low
    ]
    spread = jnp.concatenate([(hot * piece).astype(jnp.bfloat16) for piece in pieces], axis=0)
    put = lax.dot_general(
        spread, place, (((1,), (1,)), ((), ())), preferred_element_type=jnp.float32
    )
    taken = [put[i * devices:(i + 1) * devices] for i in range(5)]
    msg[:, 0, 0:LANES] = taken[0] * LANES + taken[1]
    msg[:, 0, LANES:2 * LANES] = (taken[2] + taken[3]) + taken[4]

    def message(p):
        return pltpu.make_async_remote_copy(
            src_ref=msg.at[p], dst_ref=got.at[me], send_sem=msend.at[p], recv_sem=mrecv.at[me],
            device_id=device(p), device_id_type=MESH,
        )

    def message_in(p):
        return pltpu.make_async_remote_copy(
            src_ref=msg.at[p], dst_ref=got.at[p], send_sem=msend.at[p], recv_sem=mrecv.at[p],
            device_id=device(p), device_id_type=MESH,
        )

    pl.semaphore_wait(barrier, devices - 1)
    for k in everyone:
        message(peer(k)).start()
    got[me] = msg[me]

    for load in loads:
        load.wait()
    for lane in range(lane_count):
        bsend[lane:lane + 1, :] = table[(lane + 1) * stride - 1:(lane + 1) * stride, :]

    def boundary():
        return pltpu.make_async_remote_copy(
            src_ref=bsend, dst_ref=brecv, send_sem=bsem.at[0], recv_sem=bsem.at[1],
            device_id=(lax.rem(tm + 1, tm_n), sym), device_id_type=MESH,
        )

    @pl.when(tm < tm_n - 1)
    def _():
        boundary().start()

    @pl.when(tm == 0)
    def _():
        brecv[...] = jnp.zeros_like(brecv)

    @pl.when(tm > 0)
    def _():
        boundary().wait_recv()

    edge = brecv[...]
    for lane in range(lane_count):
        table[lane * stride + PAD - 1:lane * stride + PAD, :] = edge[lane:lane + 1, :]

    rates = rates_ref[...]

    def joined(p):
        for r in range(cap):
            row = rows_s[p, 0, r]
            cur[r:r + 1, :] = table[pl.ds(row + 1, 1), :]
            prev[r:r + 1, :] = table[pl.ds(row, 1), :]
        ages = got[p, :, LANES:2 * LANES]
        ages = jnp.transpose(jnp.broadcast_to(ages, (LANES, LANES)))[:cap]
        weight = jnp.exp(-ages * rates)
        return weight * cur[...] + (1.0 - weight) * prev[...]

    def share(p, source):
        return pltpu.make_async_remote_copy(
            src_ref=sbuf.at[p],
            dst_ref=recv.at[pl.ds(pl.multiple_of(source * cap, 8), cap)],
            send_sem=jsend.at[p], recv_sem=jrecv.at[source],
            device_id=device(p), device_id_type=MESH,
        )

    for g in range(devices // group - 1, -1, -1):
        lead = peer(g * group)
        for j in range(group - 1, -1, -1):
            if g or j:
                message_in(peer(g * group + j)).wait_recv()
        whole = pl.ds(pl.multiple_of(lax.div(lead, group) * group, group), group)
        rows_v[whole] = jnp.clip(
            got[whole, :, 0:LANES].astype(jnp.int32), 0, lane_count * stride - 2
        )
        rows_copy = pltpu.make_async_copy(rows_v.at[whole], rows_s.at[whole], ssem.at[1])
        rows_copy.start()
        rows_copy.wait()

        @pl.loop(0 if g else 1, group)
        def _(j, lead=lead):
            p, bit = lead, 1
            for step in flip[:group.bit_length() - 1]:
                p = p + lax.rem(lax.div(j, bit), 2) * step
                bit *= 2
            sbuf[p] = joined(p)
            share(p, me).start()

    recv[pl.ds(pl.multiple_of(me * cap, 8), cap), :] = joined(me)
    slot_copy.wait()

    @pl.when(tm < tm_n - 1)
    def _():
        boundary().wait_send()

    for k in everyone:
        message(peer(k)).wait_send()
    for k in everyone:
        share(peer(k), peer(k)).wait_recv()

    unroll = 32

    @pl.loop(0, ticks // unroll)
    def _(b):
        start = pl.multiple_of(b * unroll, unroll)
        for u in range(unroll):
            out_ref[pl.ds(start + u, 1), :] = recv[pl.ds(slot_s[0, start + u], 1), :]

    for k in everyone:
        share(peer(k), me).wait_send()


def per_device(trade_age, trade_size, owner, symbol_lane, quote_offset, quotes, rates):
    tm_n, sym_n = lax.axis_size("tm"), lax.axis_size("sym")
    devices = tm_n * sym_n
    ticks = trade_age.shape[0]
    cap = 3 * ticks // (2 * devices)
    lane_count, quote_rows, features = quotes.shape
    vmem = pl.BlockSpec(memory_space=pltpu.VMEM)
    dma = pltpu.SemaphoreType.DMA
    joined = pl.pallas_call(
        functools.partial(join_kernel, (tm_n, sym_n, cap)),
        out_shape=jax.ShapeDtypeStruct((ticks, features), jnp.float32),
        in_specs=[vmem] * 5 + [pl.BlockSpec(memory_space=pltpu.HBM)],
        out_specs=vmem,
        scratch_shapes=[
            pltpu.VMEM((lane_count * (quote_rows + PAD), features), jnp.float32),
            pltpu.VMEM((devices * cap, features), jnp.float32),
            pltpu.VMEM((devices, cap, features), jnp.float32),
            pltpu.VMEM((devices, 1, 2 * LANES), jnp.float32),
            pltpu.VMEM((devices, 1, 2 * LANES), jnp.float32),
            pltpu.VMEM((devices, 1, LANES), jnp.int32),
            pltpu.SMEM((devices, 1, LANES), jnp.int32),
            pltpu.VMEM((1, ticks), jnp.int32),
            pltpu.SMEM((1, ticks), jnp.int32),
            pltpu.VMEM((cap, features), jnp.float32),
            pltpu.VMEM((cap, features), jnp.float32),
            pltpu.VMEM((lane_count, features), jnp.float32),
            pltpu.VMEM((lane_count, features), jnp.float32),
            dma((lane_count,)), dma((2,)),
            dma((devices,)), dma((devices,)), dma((devices,)), dma((devices,)),
            dma((2,)),
        ],
        compiler_params=pltpu.CompilerParams(
            collective_id=0, has_side_effects=True, vmem_limit_bytes=60 << 20
        ),
    )(
        owner.reshape(1, ticks), symbol_lane.reshape(1, ticks), quote_offset.reshape(1, ticks),
        trade_age.reshape(1, ticks), rates.reshape(1, features), quotes,
    )
    return trade_size[:, None] * joined


def solution(mesh):
    in_specs = (
        P(("tm", "sym")),
        P(("tm", "sym")),
        P(("tm", "sym"), None),
        P(("tm", "sym")),
        P(("tm", "sym")),
        P("sym", "tm", None),
        P(),
    )
    out_specs = P(("tm", "sym"), None)
    return jax.shard_map(
        per_device, mesh=mesh, in_specs=in_specs, out_specs=out_specs, check_vma=False
    )
```

profile of v0, /device:TPU:9, one launch (start us, length us, event | category | flops | bytes accessed | tf_op | source)
XLA Modules:
  0.0 53.7 jit_solution(6467886966804933016)
XLA Ops:
  0.0 0.0 copy-start
  0.0 51.1 %shard_map.73 = f32[2048,128]{1,0:T(8,128)} custom-call(s32[1,2048]{1,0:T(1,128)} %bitcast.5, s32[1,2048]{1,0:T(1,128)} %bitcast.6, s32[1,2048]{1,0:T(1,128)} %bitcast.7, f32[1,2048]{1,0:T(1,128)} %bitcast.8, f32[1,128]{1,0:T(1,128)} %bitcast.9, f32[16,512,128]{2,1,0:T(8,128)} %quotes_ref.1), custom_call_target="tpu_custom_call" | custom-call | tf_op jit(solution)/shard_map/pallas_call | solution.py:234
  51.1 0.0 copy-done
  51.2 2.5 %broadcast_multiply_fusion = f32[2048,128]{1,0:T(8,128)} fusion(f32[2048,128]{1,0:T(8,128)} %shard_map.73, f32[2048]{0:T(1024)S(1)} %copy-done), kind=kLoop, calls=%fused_computation | loop fusion | flops 262144 | bytes 2105344 | tf_op jit(solution)/shard_map/mul | solution.py:264
Async XLA Ops:
  0.0 51.2 %copy-start = (f32[2048]{0:T(1024)S(1)}, f32[2048]{0:T(1024)}, u32[]{:S(2)}) copy-start(f32[2048]{0:T(1024)} %param.8) | copy-start | bytes 24580
where the time goes:
time: 53.9 us; the launch traced here: 53.7 us
  Pallas kernels  51.1 us (95%)
  other arithmetic  2.53 us (5%)
    pallas_call x1, Pallas kernels, per_device(): pl.pallas_call(functools.partial(join_kernel, (tm_n, sym_n, cap)), out_sh...  51.1 us
    mul x1, other arithmetic, per_device(): return trade_size[:, None] * joined  2.53 us

commit v1 on v0

v1 whole, which is shorter than its diff:
```python
import functools

import jax
import jax.numpy as jnp
from jax import lax
from jax.experimental import pallas as pl
from jax.experimental.pallas import tpu as pltpu
from jax.sharding import PartitionSpec as P

LANES = 128
PAD = 8
PLANES = 4
BLOCK = 2048
MESH = pl.DeviceIdType.MESH


def join_kernel(
    cfg,
    owner_hbm, lane_hbm, offset_hbm, age_hbm, rates_hbm, quotes_ref,
    out_ref,
    owner_v, lane_v, offset_v, age_v, rates_v,
    table, recv, sbuf, msg_row, msg_age, got_row, got_age, key_v, cur, prev, bsend, brecv,
    isem, qsem, bsem, rsend, rrecv, asend, arecv, jsend, jrecv, relay,
):
    tm_n, sym_n, cap = cfg
    devices = tm_n * sym_n
    ticks = owner_v.shape[1]
    lane_count, quote_rows, features = quotes_ref.shape
    stride = quote_rows + PAD
    tm, sym = lax.axis_index("tm"), lax.axis_index("sym")
    me = tm * sym_n + sym

    plane_n = devices // PLANES
    bits = plane_n.bit_length() - 1
    z = lax.div(me, plane_n)
    half, quarter = lax.div(z, 2), lax.rem(z, 2)
    inner = lax.rem(half + quarter, 2)
    here = lax.rem(me, plane_n)

    def device(p):
        return (lax.div(p, sym_n), lax.rem(p, sym_n))

    def mate(j):
        q, bit = here, 1
        for _ in range(bits):
            mine = lax.rem(lax.div(here, bit), 2)
            q = q + lax.rem(lax.div(j, bit), 2) * (bit - 2 * bit * mine)
            bit *= 2
        return q

    other = 1 - half
    plane = [z, 2 * half + 1 - quarter, 2 * other + half, 2 * other + other]

    def pick(outer_g, inner_g):
        return plane[outer_g] + inner * (plane[inner_g] - plane[outer_g])

    small = [
        pltpu.make_async_copy(src, dst, isem.at[i])
        for i, (src, dst) in enumerate([
            (owner_hbm, owner_v), (lane_hbm, lane_v), (offset_hbm, offset_v), (age_hbm, age_v),
            (rates_hbm, rates_v),
        ])
    ]
    for copy in small:
        copy.start()

    barrier = pltpu.get_barrier_semaphore()

    def greet(where, first):
        @pl.loop(first, plane_n)
        def _(j):
            pl.semaphore_signal(
                barrier, inc=1, device_id=device(where * plane_n + mate(j)), device_id_type=MESH
            )

    @pl.when(z > 0)
    def _():
        greet(z - 1, 0)

    @pl.when(z < PLANES - 1)
    def _():
        greet(z + 1, 0)

    greet(z, 1)

    loads = [
        pltpu.make_async_copy(
            quotes_ref.at[lane], table.at[pl.ds(lane * stride + PAD, quote_rows)], qsem.at[lane]
        )
        for lane in range(lane_count)
    ]
    for load in loads:
        load.start()
    for copy in small:
        copy.wait()

    owner = owner_v[...]
    mine = owner == lax.broadcasted_iota(jnp.int32, (devices, ticks), 0)
    hot = mine.astype(jnp.float32)
    hot_b = hot.astype(jnp.bfloat16)
    width = 256 if ticks % 256 == 0 else 128
    upper = (
        lax.broadcasted_iota(jnp.int32, (width, width), 0)
        < lax.broadcasted_iota(jnp.int32, (width, width), 1)
    ).astype(jnp.float32).astype(jnp.bfloat16)
    base = jnp.zeros((devices, 1), jnp.float32)
    ranks = []
    for start in range(0, ticks, width):
        part = hot[:, start:start + width]
        before = jnp.dot(
            hot_b[:, start:start + width], upper, preferred_element_type=jnp.float32
        )
        ranks.append(jnp.sum(part * (before + base), axis=0, keepdims=True))
        base = base + jnp.sum(part, axis=1, keepdims=True)
    rank = jnp.concatenate(ranks, axis=1).astype(jnp.int32)
    key = owner * LANES + jnp.clip(rank, 0, cap - 1)

    place = (
        rank == lax.broadcasted_iota(jnp.int32, (LANES, ticks), 0)
    ).astype(jnp.float32).astype(jnp.bfloat16)
    local = lane_v[...] * stride + PAD - 1 + offset_v[...]
    age = age_v[...]
    high = age.astype(jnp.bfloat16).astype(jnp.float32)
    middle = (age - high).astype(jnp.bfloat16).astype(jnp.float32)
    low = age - high - middle
    pieces = [
        (local // LANES).astype(jnp.float32), (local % LANES).astype(jnp.float32), high, middle, low
    ]
    spread = jnp.concatenate([(hot * piece).astype(jnp.bfloat16) for piece in pieces], axis=0)
    put = lax.dot_general(
        spread, place, (((1,), (1,)), ((), ())), preferred_element_type=jnp.float32
    )
    taken = [put[i * devices:(i + 1) * devices] for i in range(5)]
    msg_row[:, 0, :] = jnp.clip(
        (taken[0] * LANES + taken[1]).astype(jnp.int32), PAD - 1, lane_count * stride - 2
    )
    msg_age[:, 0, :] = (taken[2] + taken[3]) + taken[4]

    def row_message(p, slot):
        return pltpu.make_async_remote_copy(
            src_ref=msg_row.at[p], dst_ref=got_row.at[slot],
            send_sem=rsend.at[p], recv_sem=rrecv.at[slot],
            device_id=device(p), device_id_type=MESH,
        )

    def age_message(p, slot):
        return pltpu.make_async_remote_copy(
            src_ref=msg_age.at[p], dst_ref=got_age.at[slot],
            send_sem=asend.at[p], recv_sem=arecv.at[slot],
            device_id=device(p), device_id_type=MESH,
        )

    def ask(where, first):
        @pl.loop(first, plane_n)
        def _(j):
            p = where * plane_n + mate(j)
            row_message(p, me).start()
            age_message(p, me).start()

    def boundary():
        return pltpu.make_async_remote_copy(
            src_ref=bsend, dst_ref=brecv, send_sem=bsem.at[0], recv_sem=bsem.at[1],
            device_id=(lax.rem(tm + 1, tm_n), sym), device_id_type=MESH,
        )

    for load in loads:
        load.wait()
    for lane in range(lane_count):
        bsend[lane:lane + 1, :] = table[(lane + 1) * stride - 1:(lane + 1) * stride, :]

    pl.semaphore_wait(barrier, plane_n - 1 + plane_n + plane_n * inner)

    def tell(where, which):
        pl.semaphore_signal(
            relay.at[which], inc=1, device_id=device(where * plane_n + here), device_id_type=MESH
        )

    @pl.when(inner == 1)
    def _():
        tell(z - 1, 0)
        tell(z + 1, 0)

    @pl.when(tm < tm_n - 1)
    def _():
        boundary().start()

    @pl.when(z > 0)
    def _():
        ask(z - 1, 0)

    @pl.when(z < PLANES - 1)
    def _():
        ask(z + 1, 0)

    ask(z, 1)

    pl.semaphore_wait(relay.at[0], 1)

    @pl.when(inner == 1)
    def _():
        tell(3 * half, 1)

    ask(z + 2 - 4 * half, 0)

    @pl.when(inner == 0)
    def _():
        pl.semaphore_wait(relay.at[1], 1)
        ask(3 - z, 0)

    own_row = pltpu.make_async_copy(msg_row.at[me], got_row.at[me], isem.at[0])
    own_row.start()

    @pl.when(tm == 0)
    def _():
        brecv[...] = jnp.zeros_like(brecv)

    @pl.when(tm > 0)
    def _():
        boundary().wait_recv()

    edge = brecv[...]
    for lane in range(lane_count):
        table[lane * stride + PAD - 1:lane * stride + PAD, :] = edge[lane:lane + 1, :]

    rates = rates_v[...]

    def joined(p, ages):
        for r in range(cap):
            row = got_row[p, 0, r]
            cur[r:r + 1, :] = table[pl.ds(row + 1, 1), :]
            prev[r:r + 1, :] = table[pl.ds(row, 1), :]
        ages = jnp.transpose(jnp.broadcast_to(ages, (LANES, LANES)))[:cap]
        weight = jnp.exp(-ages * rates)
        return weight * cur[...] + (1.0 - weight) * prev[...]

    def share(p, source):
        return pltpu.make_async_remote_copy(
            src_ref=sbuf.at[p], dst_ref=recv.at[source, pl.ds(0, cap)],
            send_sem=jsend.at[p], recv_sem=jrecv.at[source],
            device_id=device(p), device_id_type=MESH,
        )

    def serve(where, first, last):
        @pl.loop(first, last)
        def _(j):
            p = where * plane_n + mate(j)
            row_message(p, p).wait_recv()
            age_message(p, p).wait_recv()
            sbuf[p] = joined(p, got_age[p])
            share(p, me).start()

    few = plane_n // 4
    serve(pick(1, 2), 0, few)
    serve(pick(2, 3), 0, plane_n)
    serve(pick(1, 2), few, plane_n)
    serve(pick(3, 1), 0, plane_n)
    serve(z, 1, plane_n)

    own_row.wait()
    recv[me, 0:cap, :] = joined(me, msg_age[me])
    if cap < LANES:
        @pl.loop(0, devices)
        def _(p):
            recv[p, cap:, :] = jnp.zeros((LANES - cap, features), jnp.float32)

    for start in range(0, ticks, LANES):
        key_v[start:start + LANES, :] = jnp.transpose(
            jnp.broadcast_to(key[:, start:start + LANES], (LANES, LANES))
        )

    block = BLOCK if ticks % BLOCK == 0 else LANES
    slots = lax.broadcasted_iota(jnp.int32, (1, LANES), 1)

    def absorb(pa, pb, fresh):
        both = jnp.concatenate([recv[pa], recv[pb]], axis=0)
        first = both.astype(jnp.bfloat16)
        second = (both - first.astype(jnp.float32)).astype(jnp.bfloat16)
        parts = jnp.concatenate([first, second], axis=1)
        slot_a, slot_b = pa * LANES + slots, pb * LANES + slots

        @pl.loop(0, ticks // block)
        def _(b):
            rows = pl.ds(pl.multiple_of(b * block, block), block)
            keys = key_v[rows, :]
            chosen = jnp.concatenate([
                (keys == slot_a).astype(jnp.float32).astype(jnp.bfloat16),
                (keys == slot_b).astype(jnp.float32).astype(jnp.bfloat16),
            ], axis=1)
            got = jnp.dot(chosen, parts, preferred_element_type=jnp.float32)
            got = got[:, :features] + got[:, features:]
            out_ref[rows, :] = got if fresh else out_ref[rows, :] + got

    def arrived(p):
        share(p, p).wait_recv()

    partner = z * plane_n + mate(1)
    arrived(partner)
    absorb(me, partner, True)

    for where, first in (
        (z, 1), (plane[1], 0), (pick(2, 3), 0), (pick(3, 2), 0),
    ):
        @pl.loop(first, plane_n // 2)
        def _(i, where=where):
            pa = where * plane_n + mate(2 * i)
            pb = where * plane_n + mate(2 * i + 1)
            arrived(pa)
            arrived(pb)
            absorb(pa, pb, False)

    @pl.when(tm < tm_n - 1)
    def _():
        boundary().wait_send()

    def settle(where, first):
        @pl.loop(first, plane_n)
        def _(j):
            p = where * plane_n + mate(j)
            row_message(p, me).wait_send()
            age_message(p, me).wait_send()
            share(p, me).wait_send()

    settle(z, 1)
    for where in plane[1:]:
        settle(where, 0)


def per_device(trade_age, trade_size, owner, symbol_lane, quote_offset, quotes, rates):
    tm_n, sym_n = lax.axis_size("tm"), lax.axis_size("sym")
    devices = tm_n * sym_n
    ticks = trade_age.shape[0]
    cap = 3 * ticks // (2 * devices)
    lane_count, quote_rows, features = quotes.shape
    dma = pltpu.SemaphoreType.DMA
    operands = [
        pltpu.with_memory_space_constraint(x, pltpu.HBM)
        for x in (
            owner.reshape(1, ticks), symbol_lane.reshape(1, ticks),
            quote_offset.reshape(1, ticks), trade_age.reshape(1, ticks),
            rates.reshape(1, features), quotes,
        )
    ]
    joined = pl.pallas_call(
        functools.partial(join_kernel, (tm_n, sym_n, cap)),
        out_shape=jax.ShapeDtypeStruct((ticks, features), jnp.float32),
        in_specs=[pl.BlockSpec(memory_space=pltpu.HBM)] * 6,
        out_specs=pl.BlockSpec(memory_space=pltpu.VMEM),
        scratch_shapes=[
            pltpu.VMEM((1, ticks), jnp.int32),
            pltpu.VMEM((1, ticks), jnp.int32),
            pltpu.VMEM((1, ticks), jnp.int32),
            pltpu.VMEM((1, ticks), jnp.float32),
            pltpu.VMEM((1, features), jnp.float32),
            pltpu.VMEM((lane_count * (quote_rows + PAD), features), jnp.float32),
            pltpu.VMEM((devices, LANES, features), jnp.float32),
            pltpu.VMEM((devices, cap, features), jnp.float32),
            pltpu.VMEM((devices, 1, LANES), jnp.int32),
            pltpu.VMEM((devices, 1, LANES), jnp.float32),
            pltpu.SMEM((devices, 1, LANES), jnp.int32),
            pltpu.VMEM((devices, 1, LANES), jnp.float32),
            pltpu.VMEM((ticks, LANES), jnp.int32),
            pltpu.VMEM((cap, features), jnp.float32),
            pltpu.VMEM((cap, features), jnp.float32),
            pltpu.VMEM((lane_count, features), jnp.float32),
            pltpu.VMEM((lane_count, features), jnp.float32),
            dma((5,)), dma((lane_count,)), dma((2,)),
            dma((devices,)), dma((devices,)), dma((devices,)), dma((devices,)),
            dma((devices,)), dma((devices,)),
            pltpu.SemaphoreType.REGULAR((2,)),
        ],
        compiler_params=pltpu.CompilerParams(
            collective_id=0, has_side_effects=True, vmem_limit_bytes=32 << 20
        ),
    )(*operands)
    return trade_size[:, None] * joined


def solution(mesh):
    in_specs = (
        P(("tm", "sym")),
        P(("tm", "sym")),
        P(("tm", "sym"), None),
        P(("tm", "sym")),
        P(("tm", "sym")),
        P("sym", "tm", None),
        P(),
    )
    out_specs = P(("tm", "sym"), None)
    return jax.shard_map(
        per_device, mesh=mesh, in_specs=in_specs, out_specs=out_specs, check_vma=False
    )
```

time: 53.9 us -> 47.4 us (0.88)
  Pallas kernels: 51.1 us -> 45.9 us
  other arithmetic: 2.53 us -> 1.31 us
    pallas_call x1, Pallas kernels: 51.1 us -> 45.9 us  [per_device(): pl.pallas_call(functools.partial(join_kernel, (tm_n, sym_n, cap)), out_sh...]
    mul x1, other arithmetic: 2.53 us -> 1.31 us  [per_device(): return trade_size[:, None] * joined]
where the time goes in v1:
time: 47.4 us; the launch traced here: 47.2 us
  Pallas kernels  45.9 us (97%)
  other arithmetic  1.31 us (3%)
    pallas_call x1, Pallas kernels, per_device(): pl.pallas_call(functools.partial(join_kernel, (tm_n, sym_n, cap)), out_sh...  45.9 us
    mul x1, other arithmetic, per_device(): return trade_size[:, None] * joined  1.31 us

profile of v1, /device:TPU:9, one launch (start us, length us, event | category | flops | bytes accessed | tf_op | source)
XLA Modules:
  0.0 47.2 jit_solution(12464642265300596052)
XLA Ops:
  0.0 0.0 copy-start
  0.0 45.9 %shard_map.73 = f32[2048,128]{1,0:T(8,128)S(1)} custom-call(s32[1,2048]{1,0:T(1,128)} %bitcast.5, s32[1,2048]{1,0:T(1,128)} %bitcast.6, s32[1,2048]{1,0:T(1,128)} %bitcast.7, f32[1,2048]{1,0:T(1,128)} %bitcast.8, f32[1,128]{1,0:T(1,128)} %bitcast.9, f32[16,512,128]{2,1,0:T(8,128)} %quotes_ref.1), custom_call_target="tpu_custom_call" | custom-call | tf_op jit(solution)/shard_map/pallas_call | solution.py:343
  45.9 0.0 copy-done
  45.9 1.3 %broadcast_multiply_fusion = f32[2048,128]{1,0:T(8,128)} fusion(f32[2048,128]{1,0:T(8,128)S(1)} %shard_map.73, f32[2048]{0:T(1024)S(1)} %copy-done), kind=kLoop, calls=%fused_computation | loop fusion | flops 262144 | bytes 2105344 | tf_op jit(solution)/shard_map/mul | solution.py:375
Async XLA Ops:
  0.0 45.9 %copy-start = (f32[2048]{0:T(1024)S(1)}, f32[2048]{0:T(1024)}, u32[]{:S(2)}) copy-start(f32[2048]{0:T(1024)} %param.8) | copy-start | bytes 24580

commit v2 on v1

--- a/solution.py
+++ b/solution.py
@@ -16,10 +16,10 @@
 
 def join_kernel(
     cfg,
-    owner_hbm, lane_hbm, offset_hbm, age_hbm, rates_hbm, quotes_ref,
+    owner_hbm, lane_hbm, offset_hbm, age_hbm, size_hbm, rates_hbm, quotes_ref,
     out_ref,
-    owner_v, lane_v, offset_v, age_v, rates_v,
-    table, recv, sbuf, msg_row, msg_age, got_row, got_age, key_v, cur, prev, bsend, brecv,
+    owner_v, lane_v, offset_v, age_v, size_v, rates_v,
+    table, recv, sbuf, msg_row, msg_age, got_row, got_age, key_v, scale_v, cur, prev, bsend, brecv, tail,
     isem, qsem, bsem, rsend, rrecv, asend, arecv, jsend, jrecv, relay,
 ):
     tm_n, sym_n, cap = cfg
@@ -40,12 +40,15 @@
     def device(p):
         return (lax.div(p, sym_n), lax.rem(p, sym_n))
 
+    flip = [(1 << i) - (2 << i) * lax.rem(lax.div(here, 1 << i), 2) for i in range(bits)]
+
     def mate(j):
-        q, bit = here, 1
-        for _ in range(bits):
-            mine = lax.rem(lax.div(here, bit), 2)
-            q = q + lax.rem(lax.div(j, bit), 2) * (bit - 2 * bit * mine)
-            bit *= 2
+        q = here
+        for i, step in enumerate(flip):
+            if not isinstance(j, int):
+                q = q + lax.rem(lax.div(j, 1 << i), 2) * step
+            elif j >> i & 1:
+                q = q + step
         return q
 
     other = 1 - half
@@ -58,30 +61,38 @@
         pltpu.make_async_copy(src, dst, isem.at[i])
         for i, (src, dst) in enumerate([
             (owner_hbm, owner_v), (lane_hbm, lane_v), (offset_hbm, offset_v), (age_hbm, age_v),
-            (rates_hbm, rates_v),
+            (rates_hbm, rates_v), (size_hbm, size_v),
         ])
     ]
+    last_rows = pltpu.make_async_copy(
+        quotes_ref.at[:, pl.ds(quote_rows - PAD, PAD)], tail, isem.at[6]
+    )
     for copy in small:
         copy.start()
+    last_rows.start()
 
     barrier = pltpu.get_barrier_semaphore()
 
-    def greet(where, first):
-        @pl.loop(first, plane_n)
-        def _(j):
-            pl.semaphore_signal(
-                barrier, inc=1, device_id=device(where * plane_n + mate(j)), device_id_type=MESH
-            )
-
-    @pl.when(z > 0)
-    def _():
-        greet(z - 1, 0)
-
-    @pl.when(z < PLANES - 1)
-    def _():
-        greet(z + 1, 0)
-
-    greet(z, 1)
+    def greet(p):
+        pl.semaphore_signal(barrier, inc=1, device_id=device(p), device_id_type=MESH)
+
+    rows_n = tm_n // PLANES
+    first_row = 1 - lax.div(lax.rem(tm, rows_n) + rows_n - 1, rows_n)
+    last_row = lax.div(lax.rem(tm, rows_n) + 1, rows_n)
+
+    @pl.when(inner == 1)
+    def _():
+        for j in range(plane_n):
+            greet(plane[2] * plane_n + mate(j))
+        for j in range(plane_n):
+            greet(plane[1] * plane_n + mate(j))
+
+    @pl.when(inner == 0)
+    def _():
+        greet(plane[1] * plane_n + here)
+
+    for j in range(plane_n - 1, 0, -1):
+        greet(z * plane_n + mate(j))
 
     loads = [
         pltpu.make_async_copy(
@@ -139,20 +150,19 @@
     def row_message(p, slot):
         return pltpu.make_async_remote_copy(
             src_ref=msg_row.at[p], dst_ref=got_row.at[slot],
-            send_sem=rsend.at[p], recv_sem=rrecv.at[slot],
+            send_sem=rsend, recv_sem=rrecv.at[slot],
             device_id=device(p), device_id_type=MESH,
         )
 
     def age_message(p, slot):
         return pltpu.make_async_remote_copy(
             src_ref=msg_age.at[p], dst_ref=got_age.at[slot],
-            send_sem=asend.at[p], recv_sem=arecv.at[slot],
+            send_sem=asend, recv_sem=arecv.at[slot],
             device_id=device(p), device_id_type=MESH,
         )
 
-    def ask(where, first):
-        @pl.loop(first, plane_n)
-        def _(j):
+    def ask(where, first, last):
+        for j in range(first, last):
             p = where * plane_n + mate(j)
             row_message(p, me).start()
             age_message(p, me).start()
@@ -163,49 +173,52 @@
             device_id=(lax.rem(tm + 1, tm_n), sym), device_id_type=MESH,
         )
 
-    for load in loads:
-        load.wait()
+    last_rows.wait()
     for lane in range(lane_count):
-        bsend[lane:lane + 1, :] = table[(lane + 1) * stride - 1:(lane + 1) * stride, :]
-
-    pl.semaphore_wait(barrier, plane_n - 1 + plane_n + plane_n * inner)
+        bsend[lane:lane + 1, :] = tail[lane, PAD - 1:PAD, :]
 
     def tell(where, which):
         pl.semaphore_signal(
             relay.at[which], inc=1, device_id=device(where * plane_n + here), device_id_type=MESH
         )
 
+    def heard(which):
+        pl.semaphore_wait(relay.at[which], 1)
+
+    near = pick(1, 2)
+
+    pl.semaphore_wait(barrier, 2 * plane_n - 1 + inner)
+
+    @pl.when(last_row * half == 0)
+    def _():
+        boundary().start()
+
+    ask(near, 0, plane_n)
+
     @pl.when(inner == 1)
     def _():
-        tell(z - 1, 0)
-        tell(z + 1, 0)
-
-    @pl.when(tm < tm_n - 1)
-    def _():
-        boundary().start()
-
-    @pl.when(z > 0)
-    def _():
-        ask(z - 1, 0)
-
-    @pl.when(z < PLANES - 1)
-    def _():
-        ask(z + 1, 0)
-
-    ask(z, 1)
-
-    pl.semaphore_wait(relay.at[0], 1)
-
-    @pl.when(inner == 1)
-    def _():
-        tell(3 * half, 1)
-
-    ask(z + 2 - 4 * half, 0)
+        tell(plane[1], 1)
+        heard(1)
+        tell(plane[2], 2)
+
+        @pl.when(last_row * half == 1)
+        def _():
+            boundary().start()
+
+        ask(plane[1], 0, plane_n)
+        heard(2)
+        tell(plane[1], 2)
+        ask(plane[3], 0, plane_n)
 
     @pl.when(inner == 0)
     def _():
-        pl.semaphore_wait(relay.at[1], 1)
-        ask(3 - z, 0)
+        tell(plane[1], 1)
+        heard(1)
+        ask(plane[2], 0, plane_n)
+        heard(2)
+        ask(plane[3], 0, plane_n)
+
+    ask(z, 1, plane_n)
 
     own_row = pltpu.make_async_copy(msg_row.at[me], got_row.at[me], isem.at[0])
     own_row.start()
@@ -218,6 +231,8 @@
     def _():
         boundary().wait_recv()
 
+    for load in loads:
+        load.wait()
     edge = brecv[...]
     for lane in range(lane_count):
         table[lane * stride + PAD - 1:lane * stride + PAD, :] = edge[lane:lane + 1, :]
@@ -236,9 +251,15 @@
     def share(p, source):
         return pltpu.make_async_remote_copy(
             src_ref=sbuf.at[p], dst_ref=recv.at[source, pl.ds(0, cap)],
-            send_sem=jsend.at[p], recv_sem=jrecv.at[source],
+            send_sem=jsend, recv_sem=jrecv.at[source],
             device_id=device(p), device_id_type=MESH,
         )
+
+    def sent(src, dst, sem):
+        pltpu.make_async_remote_copy(
+            src_ref=src.at[pl.ds(0, devices - 1)], dst_ref=dst, send_sem=sem,
+            recv_sem=jrecv.at[0], device_id=device(z * plane_n + mate(1)), device_id_type=MESH,
+        ).wait_send()
 
     def serve(where, first, last):
         @pl.loop(first, last)
@@ -256,6 +277,8 @@
     serve(pick(3, 1), 0, plane_n)
     serve(z, 1, plane_n)
 
+    sent(msg_row, got_row.at[pl.ds(0, devices - 1)], rsend)
+    sent(msg_age, got_age.at[pl.ds(0, devices - 1)], asend)
     own_row.wait()
     recv[me, 0:cap, :] = joined(me, msg_age[me])
     if cap < LANES:
@@ -267,11 +290,14 @@
         key_v[start:start + LANES, :] = jnp.transpose(
             jnp.broadcast_to(key[:, start:start + LANES], (LANES, LANES))
         )
+        scale_v[start:start + LANES, :] = jnp.transpose(
+            jnp.broadcast_to(size_v[:, start:start + LANES], (LANES, LANES))
+        )
 
     block = BLOCK if ticks % BLOCK == 0 else LANES
     slots = lax.broadcasted_iota(jnp.int32, (1, LANES), 1)
 
-    def absorb(pa, pb, fresh):
+    def absorb(pa, pb, fresh=False, final=False):
         both = jnp.concatenate([recv[pa], recv[pb]], axis=0)
         first = both.astype(jnp.bfloat16)
         second = (both - first.astype(jnp.float32)).astype(jnp.bfloat16)
@@ -288,41 +314,40 @@
             ], axis=1)
             got = jnp.dot(chosen, parts, preferred_element_type=jnp.float32)
             got = got[:, :features] + got[:, features:]
-            out_ref[rows, :] = got if fresh else out_ref[rows, :] + got
+            if not fresh:
+                got = out_ref[rows, :] + got
+            out_ref[rows, :] = got * scale_v[rows, :] if final else got
 
     def arrived(p):
         share(p, p).wait_recv()
 
     partner = z * plane_n + mate(1)
     arrived(partner)
-    absorb(me, partner, True)
-
-    for where, first in (
-        (z, 1), (plane[1], 0), (pick(2, 3), 0), (pick(3, 2), 0),
+    absorb(me, partner, fresh=True)
+
+    def collect(where, i, final=False):
+        pa = where * plane_n + mate(2 * i)
+        pb = where * plane_n + mate(2 * i + 1)
+        arrived(pa)
+        arrived(pb)
+        absorb(pa, pb, final=final)
+
+    pairs = plane_n // 2
+    last = pick(3, 2)
+    for where, first, stop in (
+        (z, 1, pairs), (plane[1], 0, pairs), (pick(2, 3), 0, pairs), (last, 0, pairs - 1),
     ):
-        @pl.loop(first, plane_n // 2)
+        @pl.loop(first, stop)
         def _(i, where=where):
-            pa = where * plane_n + mate(2 * i)
-            pb = where * plane_n + mate(2 * i + 1)
-            arrived(pa)
-            arrived(pb)
-            absorb(pa, pb, False)
+            collect(where, i)
+
+    collect(last, pairs - 1, True)
 
     @pl.when(tm < tm_n - 1)
     def _():
         boundary().wait_send()
 
-    def settle(where, first):
-        @pl.loop(first, plane_n)
-        def _(j):
-            p = where * plane_n + mate(j)
-            row_message(p, me).wait_send()
-            age_message(p, me).wait_send()
-            share(p, me).wait_send()
-
-    settle(z, 1)
-    for where in plane[1:]:
-        settle(where, 0)
+    sent(sbuf, recv.at[pl.ds(0, devices - 1), pl.ds(0, cap)], jsend)
 
 
 def per_device(trade_age, trade_size, owner, symbol_lane, quote_offset, quotes, rates):
@@ -337,18 +362,20 @@
         for x in (
             owner.reshape(1, ticks), symbol_lane.reshape(1, ticks),
             quote_offset.reshape(1, ticks), trade_age.reshape(1, ticks),
+            trade_size.reshape(1, ticks),
             rates.reshape(1, features), quotes,
         )
     ]
     joined = pl.pallas_call(
         functools.partial(join_kernel, (tm_n, sym_n, cap)),
         out_shape=jax.ShapeDtypeStruct((ticks, features), jnp.float32),
-        in_specs=[pl.BlockSpec(memory_space=pltpu.HBM)] * 6,
+        in_specs=[pl.BlockSpec(memory_space=pltpu.HBM)] * 7,
         out_specs=pl.BlockSpec(memory_space=pltpu.VMEM),
         scratch_shapes=[
             pltpu.VMEM((1, ticks), jnp.int32),
             pltpu.VMEM((1, ticks), jnp.int32),
             pltpu.VMEM((1, ticks), jnp.int32),
+            pltpu.VMEM((1, ticks), jnp.float32),
             pltpu.VMEM((1, ticks), jnp.float32),
             pltpu.VMEM((1, features), jnp.float32),
             pltpu.VMEM((lane_count * (quote_rows + PAD), features), jnp.float32),
@@ -359,20 +386,21 @@
             pltpu.SMEM((devices, 1, LANES), jnp.int32),
             pltpu.VMEM((devices, 1, LANES), jnp.float32),
             pltpu.VMEM((ticks, LANES), jnp.int32),
+            pltpu.VMEM((ticks, features), jnp.float32),
             pltpu.VMEM((cap, features), jnp.float32),
             pltpu.VMEM((cap, features), jnp.float32),
             pltpu.VMEM((lane_count, features), jnp.float32),
             pltpu.VMEM((lane_count, features), jnp.float32),
-            dma((5,)), dma((lane_count,)), dma((2,)),
-            dma((devices,)), dma((devices,)), dma((devices,)), dma((devices,)),
-            dma((devices,)), dma((devices,)),
-            pltpu.SemaphoreType.REGULAR((2,)),
+            pltpu.VMEM((lane_count, PAD, features), jnp.float32),
+            dma((7,)), dma((lane_count,)), dma((2,)),
+            dma, dma((devices,)), dma, dma((devices,)), dma, dma((devices,)),
+            pltpu.SemaphoreType.REGULAR((3,)),
         ],
         compiler_params=pltpu.CompilerParams(
             collective_id=0, has_side_effects=True, vmem_limit_bytes=32 << 20
         ),
     )(*operands)
-    return trade_size[:, None] * joined
+    return joined
 
 
 def solution(mesh):

time: 47.4 us -> 44.5 us (0.939)
  Pallas kernels: 45.9 us -> 43.4 us
  other arithmetic: 1.31 us -> 0 us
  local copies, waits for them, and re-layouts: 0.01 us -> 0.97 us
    pallas_call x1, Pallas kernels: 45.9 us -> 43.4 us  [per_device(): pl.pallas_call(functools.partial(join_kernel, (tm_n, sym_n, cap)), out_sh...]
    mul x1 -> x0, other arithmetic: 1.31 us -> none  [per_device(): return trade_size[:, None] * joined]
    unnamed x2 -> x1, local copies, waits for them, and re-layouts: 0.01 us -> 0.97 us
where the time goes in v2:
time: 44.5 us; the launch traced here: 44.3 us
  Pallas kernels  43.4 us (98%)
  local copies, waits for them, and re-layouts  0.97 us (2%)
    pallas_call x1, Pallas kernels, per_device(): pl.pallas_call(functools.partial(join_kernel, (tm_n, sym_n, cap)), out_sh...  43.4 us
    unnamed x1, local copies, waits for them, and re-layouts  0.97 us

profile of v2, /device:TPU:9, one launch (start us, length us, event | category | flops | bytes accessed | tf_op | source)
XLA Modules:
  0.0 44.3 jit_solution(3792680192382373321)
XLA Ops:
  0.0 43.4 %shard_map.73 = f32[2048,128]{1,0:T(8,128)S(1)} custom-call(s32[1,2048]{1,0:T(1,128)} %bitcast.6, s32[1,2048]{1,0:T(1,128)} %bitcast.7, s32[1,2048]{1,0:T(1,128)} %bitcast.8, f32[1,2048]{1,0:T(1,128)} %bitcast.9, f32[1,2048]{1,0:T(1,128)} %bitcast.10, f32[1,128]{1,0:T(1,128)} %bitcast.11, f32[16,512,128]{2,1,0:T(8,128)} %quotes_ref.1), custom_call_target="tpu_custom_call" | custom-call | tf_op jit(solution)/shard_map/pallas_call | solution.py:369
  43.4 1.0 %copy.9 = f32[2048,128]{1,0:T(8,128)} copy(f32[2048,128]{1,0:T(8,128)S(1)} %shard_map.73) | data formatting | bytes 2097152

commit v3 on v2

--- a/solution.py
+++ b/solution.py
@@ -16,11 +16,11 @@
 
 def join_kernel(
     cfg,
-    owner_hbm, lane_hbm, offset_hbm, age_hbm, size_hbm, rates_hbm, quotes_ref,
+    owner_hbm, lane_hbm, offset_hbm, age_hbm, size_hbm, rates_hbm, quotes_ref, quotes_flat,
     out_ref,
     owner_v, lane_v, offset_v, age_v, size_v, rates_v,
     table, recv, sbuf, msg_row, msg_age, got_row, got_age, key_v, scale_v, cur, prev, bsend, brecv, tail,
-    isem, qsem, bsem, rsend, rrecv, asend, arecv, jsend, jrecv, relay,
+    isem, qsem, bsem, rsend, rrecv, arecv, jsend, jrecv, relay,
 ):
     tm_n, sym_n, cap = cfg
     devices = tm_n * sym_n
@@ -96,7 +96,7 @@
 
     loads = [
         pltpu.make_async_copy(
-            quotes_ref.at[lane], table.at[pl.ds(lane * stride + PAD, quote_rows)], qsem.at[lane]
+            quotes_ref.at[lane], table.at[pl.ds(lane * stride + PAD, quote_rows)], qsem
         )
         for lane in range(lane_count)
     ]
@@ -157,7 +157,7 @@
     def age_message(p, slot):
         return pltpu.make_async_remote_copy(
             src_ref=msg_age.at[p], dst_ref=got_age.at[slot],
-            send_sem=asend, recv_sem=arecv.at[slot],
+            send_sem=rsend, recv_sem=arecv.at[slot],
             device_id=device(p), device_id_type=MESH,
         )
 
@@ -231,8 +231,9 @@
     def _():
         boundary().wait_recv()
 
-    for load in loads:
-        load.wait()
+    pltpu.make_async_copy(
+        quotes_flat, table.at[pl.ds(0, lane_count * quote_rows)], qsem
+    ).wait()
     edge = brecv[...]
     for lane in range(lane_count):
         table[lane * stride + PAD - 1:lane * stride + PAD, :] = edge[lane:lane + 1, :]
@@ -251,7 +252,7 @@
     def share(p, source):
         return pltpu.make_async_remote_copy(
             src_ref=sbuf.at[p], dst_ref=recv.at[source, pl.ds(0, cap)],
-            send_sem=jsend, recv_sem=jrecv.at[source],
+            send_sem=jsend, recv_sem=jrecv.at[lax.div(source, 2)],
             device_id=device(p), device_id_type=MESH,
         )
 
@@ -277,8 +278,12 @@
     serve(pick(3, 1), 0, plane_n)
     serve(z, 1, plane_n)
 
-    sent(msg_row, got_row.at[pl.ds(0, devices - 1)], rsend)
-    sent(msg_age, got_age.at[pl.ds(0, devices - 1)], asend)
+    @pl.when(tm < tm_n - 1)
+    def _():
+        boundary().wait_send()
+
+    sent(msg_age, got_age.at[pl.ds(0, devices - 1)], rsend)
+    sent(msg_age, got_age.at[pl.ds(0, devices - 1)], rsend)
     own_row.wait()
     recv[me, 0:cap, :] = joined(me, msg_age[me])
     if cap < LANES:
@@ -318,18 +323,22 @@
                 got = out_ref[rows, :] + got
             out_ref[rows, :] = got * scale_v[rows, :] if final else got
 
-    def arrived(p):
-        share(p, p).wait_recv()
+    def both_shares(pair):
+        two = pl.ds(2 * pair, 2)
+        return pltpu.make_async_remote_copy(
+            src_ref=sbuf.at[two], dst_ref=recv.at[two, pl.ds(0, cap)],
+            send_sem=jsend, recv_sem=jrecv.at[pair],
+            device_id=device(2 * pair), device_id_type=MESH,
+        )
 
     partner = z * plane_n + mate(1)
-    arrived(partner)
+    share(partner, partner).wait_recv()
     absorb(me, partner, fresh=True)
 
     def collect(where, i, final=False):
         pa = where * plane_n + mate(2 * i)
         pb = where * plane_n + mate(2 * i + 1)
-        arrived(pa)
-        arrived(pb)
+        both_shares(lax.div(pa, 2)).wait_recv()
         absorb(pa, pb, final=final)
 
     pairs = plane_n // 2
@@ -342,10 +351,6 @@
             collect(where, i)
 
     collect(last, pairs - 1, True)
-
-    @pl.when(tm < tm_n - 1)
-    def _():
-        boundary().wait_send()
 
     sent(sbuf, recv.at[pl.ds(0, devices - 1), pl.ds(0, cap)], jsend)
 
@@ -363,13 +368,13 @@
             owner.reshape(1, ticks), symbol_lane.reshape(1, ticks),
             quote_offset.reshape(1, ticks), trade_age.reshape(1, ticks),
             trade_size.reshape(1, ticks),
-            rates.reshape(1, features), quotes,
+            rates.reshape(1, features), quotes, quotes.reshape(-1, features),
         )
     ]
     joined = pl.pallas_call(
         functools.partial(join_kernel, (tm_n, sym_n, cap)),
         out_shape=jax.ShapeDtypeStruct((ticks, features), jnp.float32),
-        in_specs=[pl.BlockSpec(memory_space=pltpu.HBM)] * 7,
+        in_specs=[pl.BlockSpec(memory_space=pltpu.HBM)] * 8,
         out_specs=pl.BlockSpec(memory_space=pltpu.VMEM),
         scratch_shapes=[
             pltpu.VMEM((1, ticks), jnp.int32),
@@ -392,8 +397,8 @@
             pltpu.VMEM((lane_count, features), jnp.float32),
             pltpu.VMEM((lane_count, features), jnp.float32),
             pltpu.VMEM((lane_count, PAD, features), jnp.float32),
-            dma((7,)), dma((lane_count,)), dma((2,)),
-            dma, dma((devices,)), dma, dma((devices,)), dma, dma((devices,)),
+            dma((7,)), dma, dma((2,)),
+            dma, dma((devices,)), dma((devices,)), dma, dma((devices // 2,)),
             pltpu.SemaphoreType.REGULAR((3,)),
         ],
         compiler_params=pltpu.CompilerParams(

time: 44.5 us -> 44.2 us (level)
  no operation moved by 1% of the time
where the time goes in v3:
time: 44.2 us; the launch traced here: 44 us
  Pallas kernels  43 us (97%)
  local copies, waits for them, and re-layouts  0.97 us (2%)
    pallas_call x1, Pallas kernels, per_device(): pl.pallas_call(functools.partial(join_kernel, (tm_n, sym_n, cap)), out_sh...  43 us
    unnamed x1, local copies, waits for them, and re-layouts  0.97 us

profile of v3, /device:TPU:9, one launch (start us, length us, event | category | flops | bytes accessed | tf_op | source)
XLA Modules:
  0.0 44.0 jit_solution(1036639828010667182)
XLA Ops:
  0.0 43.0 %shard_map.73 = f32[2048,128]{1,0:T(8,128)S(1)} custom-call(s32[1,2048]{1,0:T(1,128)} %bitcast.8, s32[1,2048]{1,0:T(1,128)} %bitcast.9, s32[1,2048]{1,0:T(1,128)} %bitcast.10, f32[1,2048]{1,0:T(1,128)} %bitcast.11, f32[1,2048]{1,0:T(1,128)} %bitcast.12, f32[1,128]{1,0:T(1,128)} %bitcast.13, f32[16,512,128]{2,1,0:T(8,128)} %quotes_ref.1, f32[8192,128]{1,0:T(8,128)} %bitcast.7), custom_call_target="tpu_custom_call" | custom-call | tf_op jit(solution)/shard_map/pallas_call | solution.py:374
  43.1 1.0 %copy.9 = f32[2048,128]{1,0:T(8,128)} copy(f32[2048,128]{1,0:T(8,128)S(1)} %shard_map.73) | data formatting | bytes 2097152

commit v4 on v3

--- a/solution.py
+++ b/solution.py
@@ -11,15 +11,16 @@
 PAD = 8
 PLANES = 4
 BLOCK = 2048
+STORES = 4
 MESH = pl.DeviceIdType.MESH
 
 
 def join_kernel(
     cfg,
     owner_hbm, lane_hbm, offset_hbm, age_hbm, size_hbm, rates_hbm, quotes_ref, quotes_flat,
-    out_ref,
+    out_ref, pair_ref, place_v, scale_v,
     owner_v, lane_v, offset_v, age_v, size_v, rates_v,
-    table, recv, sbuf, msg_row, msg_age, got_row, got_age, key_v, scale_v, cur, prev, bsend, brecv, tail,
+    table, recv, sbuf, msg_row, msg_age, got_row, got_age, key_v, cur, prev, bsend, brecv, tail,
     isem, qsem, bsem, rsend, rrecv, arecv, jsend, jrecv, relay,
 ):
     tm_n, sym_n, cap = cfg
@@ -291,10 +292,14 @@
         def _(p):
             recv[p, cap:, :] = jnp.zeros((LANES - cap, features), jnp.float32)
 
+    pairs = plane_n // 2
+    last = pick(3, 2)
+    chip = lax.div(last * plane_n + mate(plane_n - 1), 2)
     for start in range(0, ticks, LANES):
         key_v[start:start + LANES, :] = jnp.transpose(
             jnp.broadcast_to(key[:, start:start + LANES], (LANES, LANES))
         )
+        place_v[start:start + LANES, :] = key_v[start:start + LANES, :] - chip * (2 * LANES)
         scale_v[start:start + LANES, :] = jnp.transpose(
             jnp.broadcast_to(size_v[:, start:start + LANES], (LANES, LANES))
         )
@@ -302,7 +307,7 @@
     block = BLOCK if ticks % BLOCK == 0 else LANES
     slots = lax.broadcasted_iota(jnp.int32, (1, LANES), 1)
 
-    def absorb(pa, pb, fresh=False, final=False):
+    def absorb(pa, pb, fresh=False):
         both = jnp.concatenate([recv[pa], recv[pb]], axis=0)
         first = both.astype(jnp.bfloat16)
         second = (both - first.astype(jnp.float32)).astype(jnp.bfloat16)
@@ -321,7 +326,7 @@
             got = got[:, :features] + got[:, features:]
             if not fresh:
                 got = out_ref[rows, :] + got
-            out_ref[rows, :] = got * scale_v[rows, :] if final else got
+            out_ref[rows, :] = got
 
     def both_shares(pair):
         two = pl.ds(2 * pair, 2)
@@ -335,14 +340,12 @@
     share(partner, partner).wait_recv()
     absorb(me, partner, fresh=True)
 
-    def collect(where, i, final=False):
+    def collect(where, i):
         pa = where * plane_n + mate(2 * i)
         pb = where * plane_n + mate(2 * i + 1)
         both_shares(lax.div(pa, 2)).wait_recv()
-        absorb(pa, pb, final=final)
-
-    pairs = plane_n // 2
-    last = pick(3, 2)
+        absorb(pa, pb)
+
     for where, first, stop in (
         (z, 1, pairs), (plane[1], 0, pairs), (pick(2, 3), 0, pairs), (last, 0, pairs - 1),
     ):
@@ -350,9 +353,36 @@
         def _(i, where=where):
             collect(where, i)
 
-    collect(last, pairs - 1, True)
+    both_shares(chip).wait_recv()
+    pair_ref[0:LANES, :] = recv[2 * chip]
+    pair_ref[LANES:, :] = recv[2 * chip + 1]
 
     sent(sbuf, recv.at[pl.ds(0, devices - 1), pl.ds(0, cap)], jsend)
+
+
+def store_kernel(joined_ref, pair_ref, place_ref, scale_ref, out_ref, done_v, sem):
+    ticks, features = joined_ref.shape
+    block = ticks // STORES
+    both = pair_ref[...]
+    first = both.astype(jnp.bfloat16)
+    second = (both - first.astype(jnp.float32)).astype(jnp.bfloat16)
+    parts = jnp.concatenate([first, second], axis=1)
+    slots = lax.broadcasted_iota(jnp.int32, (1, LANES), 1)
+    copies = []
+    for i in range(STORES):
+        rows = pl.ds(i * block, block)
+        place = place_ref[rows, :]
+        chosen = jnp.concatenate([
+            (place == slots).astype(jnp.float32).astype(jnp.bfloat16),
+            (place == slots + LANES).astype(jnp.float32).astype(jnp.bfloat16),
+        ], axis=1)
+        got = jnp.dot(chosen, parts, preferred_element_type=jnp.float32)
+        got = joined_ref[rows, :] + (got[:, :features] + got[:, features:])
+        done_v[rows, :] = got * scale_ref[rows, :]
+        copies.append(pltpu.make_async_copy(done_v.at[rows], out_ref.at[rows], sem.at[i]))
+        copies[-1].start()
+    for copy in copies:
+        copy.wait()
 
 
 def per_device(trade_age, trade_size, owner, symbol_lane, quote_offset, quotes, rates):
@@ -371,11 +401,16 @@
             rates.reshape(1, features), quotes, quotes.reshape(-1, features),
         )
     ]
-    joined = pl.pallas_call(
+    parts = pl.pallas_call(
         functools.partial(join_kernel, (tm_n, sym_n, cap)),
-        out_shape=jax.ShapeDtypeStruct((ticks, features), jnp.float32),
+        out_shape=[
+            jax.ShapeDtypeStruct((ticks, features), jnp.float32),
+            jax.ShapeDtypeStruct((2 * LANES, features), jnp.float32),
+            jax.ShapeDtypeStruct((ticks, LANES), jnp.int32),
+            jax.ShapeDtypeStruct((ticks, features), jnp.float32),
+        ],
         in_specs=[pl.BlockSpec(memory_space=pltpu.HBM)] * 8,
-        out_specs=pl.BlockSpec(memory_space=pltpu.VMEM),
+        out_specs=[pl.BlockSpec(memory_space=pltpu.VMEM)] * 4,
         scratch_shapes=[
             pltpu.VMEM((1, ticks), jnp.int32),
             pltpu.VMEM((1, ticks), jnp.int32),
@@ -391,7 +426,6 @@
             pltpu.SMEM((devices, 1, LANES), jnp.int32),
             pltpu.VMEM((devices, 1, LANES), jnp.float32),
             pltpu.VMEM((ticks, LANES), jnp.int32),
-            pltpu.VMEM((ticks, features), jnp.float32),
             pltpu.VMEM((cap, features), jnp.float32),
             pltpu.VMEM((cap, features), jnp.float32),
             pltpu.VMEM((lane_count, features), jnp.float32),
@@ -405,7 +439,14 @@
             collective_id=0, has_side_effects=True, vmem_limit_bytes=32 << 20
         ),
     )(*operands)
-    return joined
+    return pl.pallas_call(
+        store_kernel,
+        out_shape=jax.ShapeDtypeStruct((ticks, features), jnp.float32),
+        in_specs=[pl.BlockSpec(memory_space=pltpu.VMEM)] * 4,
+        out_specs=pl.BlockSpec(memory_space=pltpu.HBM),
+        scratch_shapes=[pltpu.VMEM((ticks, features), jnp.float32), dma((STORES,))],
+        compiler_params=pltpu.CompilerParams(vmem_limit_bytes=16 << 20),
+    )(*parts)
 
 
 def solution(mesh):

time: 44.2 us -> 44.1 us (level)
  local copies, waits for them, and re-layouts: 0.97 us -> 0 us
  Pallas kernels: 43 us -> 43.9 us
    pallas_call x0 -> x1, Pallas kernels: none -> 1.32 us  [per_device(): pl.pallas_call(store_kernel, out_shape=jax.ShapeDtypeStruct((ticks, featu...]
    unnamed x1 -> x0, local copies, waits for them, and re-layouts: 0.97 us -> none
where the time goes in v4:
time: 44.1 us; the launch traced here: 43.9 us
  Pallas kernels  43.9 us (100%)
    pallas_call x1, Pallas kernels, per_device(): pl.pallas_call(functools.partial(join_kernel, (tm_n, sym_n, cap)), out_sh...  42.6 us
    pallas_call x1, Pallas kernels, per_device(): pl.pallas_call(store_kernel, out_shape=jax.ShapeDtypeStruct((ticks, featu...  1.32 us

profile of v4, /device:TPU:9, one launch (start us, length us, event | category | flops | bytes accessed | tf_op | source)
XLA Modules:
  0.0 43.9 jit_solution(513618111693146923)
XLA Ops:
  0.0 42.6 %shard_map.73 = (f32[2048,128]{1,0:T(8,128)S(1)}, f32[256,128]{1,0:T(8,128)S(1)}, s32[2048,128]{1,0:T(8,128)S(1)}, f32[2048,128]{1,0:T(8,128)S(1)}) custom-call(s32[1,2048]{1,0:T(1,128)} %bitcast.8, s32[1,2048]{1,0:T(1,128)} %bitcast.9, s32[1,2048]{1,0:T(1,128)} %bitcast.10, f32[1,2048]{1,0:T(1,128)} %bitcast.11, f32[1,2048]{1,0:T(1,128)} %bitcast.12, ...), custom_call_target="tpu_custom_call" | custom-call | tf_op jit(solution)/shard_map/pallas_call | solution.py:404
  42.6 1.3 %shard_map.74 = f32[2048,128]{1,0:T(8,128)} custom-call(f32[2048,128]{1,0:T(8,128)S(1)} %get-tuple-element.9.joined_ref, f32[256,128]{1,0:T(8,128)S(1)} %get-tuple-element.10.pair_ref, s32[2048,128]{1,0:T(8,128)S(1)} %get-tuple-element.11.place_ref, f32[2048,128]{1,0:T(8,128)S(1)} %get-tuple-element.12.scale_ref), custom_call_target="tpu_custom_call" | custom-call | tf_op jit(solution)/shard_map/pallas_call | solution.py:442
